TPU v7x, 8 devices: a whole 2x2x1 slice. The times are simulated.
8 devices in a mesh: dp: 2 (over z, y), vp: 4 (over x, core).
Axes of the slice: x: 2, y: 2, z: 1, core: 2. Of those that a mesh axis runs over, the one named last changes fastest.
Arguments:
- hidden: bfloat16 [512, 12288], P('dp'), parts along dimension 0
- w_head: bfloat16 [12288, 32768], P(None, 'vp')
- inv_temp: float32 [512], P('dp'), parts along dimension 0
- target_ids: int32 [512], P('dp'), parts along dimension 0
Outputs:
- output 1: float32 [512, 32768], P(('dp', 'vp')), parts along dimension 0
- output 2: float32 [512], P('dp'), parts along dimension 0
There are 2 independent parts. A program takes and returns all parts, laid end to end along the dimension named above; an argument that names none is the same for every part.
All inputs are finite; a program needn't handle non-finite values.
Results may differ from a plain program's by a relative error of at most 0.001.
Values are sent between devices in bfloat16 or wider.
A program may use at most 1 GiB of HBM per device.

v0:
```python
import jax
import jax.numpy as jnp
from jax import lax
from jax.sharding import PartitionSpec as P, NamedSharding


def solution(mesh):
    group_size = mesh.shape["vp"]

    def local_step(hidden, w_local, inv_temp, target_ids):
        group_index = lax.axis_index("vp")
        local_vocab = w_local.shape[1]
        logits = jnp.dot(hidden, w_local, preferred_element_type=jnp.float32)
        scaled = logits * inv_temp[:, None]
        local_max = jnp.max(scaled, axis=1)
        exp_vals = jnp.exp(scaled - local_max[:, None])
        local_sum = jnp.sum(exp_vals, axis=1)
        shard_stats = lax.all_gather(jnp.stack([local_max, local_sum]), "vp")
        global_max = jnp.max(shard_stats[:, 0], axis=0)
        global_sum = jnp.sum(shard_stats[:, 1] * jnp.exp(shard_stats[:, 0] - global_max[None, :]), axis=0)
        row_scale = jnp.exp(local_max - global_max) / global_sum
        local_cdf = jnp.cumsum(exp_vals * row_scale[:, None], axis=1)
        totals = lax.all_gather(local_cdf[:, -1], "vp")
        earlier = (jnp.arange(group_size) < group_index)[:, None]
        offset = jnp.sum(jnp.where(earlier, totals, 0.0), axis=0)
        cdf_cols = local_cdf + offset[:, None]
        local_ids = target_ids - group_index * local_vocab
        in_shard = (local_ids >= 0) & (local_ids < local_vocab)
        picked = jnp.take_along_axis(cdf_cols, jnp.clip(local_ids, 0, local_vocab - 1)[:, None], axis=1)[:, 0]
        cdf_at_target = lax.psum(jnp.where(in_shard, picked, 0.0), "vp")
        cdf_rows = lax.all_to_all(cdf_cols, "vp", 0, 1, tiled=True)
        return cdf_rows, cdf_at_target

    return jax.shard_map(
        local_step,
        mesh=mesh,
        in_specs=(P("dp", None), P(None, "vp"), P("dp"), P("dp")),
        out_specs=(P(("dp", "vp"), None), P("dp")),
        check_vma=False,
    )
```

profile of v0, /device:TPU:0, one launch (start us, length us, event | category | flops | bytes accessed | tf_op | source)
XLA Modules:
  0.0 275.7 jit_solution(15136651971059651955)
XLA Ops:
  0.6 76.6 %fusion.7 = (f32[256]{0:T(256)S(1)}, f32[256,8192]{1,0:T(8,128)}) fusion(f32[256]{0:T(256)} %param.6, bf16[256,12288]{1,0:T(8,128)(2,1)} %param.4, bf16[12288,8192]{1,0:T(8,128)(2,1)} %param.5), kind=kOutput, calls=%fused_computation.28 | convolution fusion | flops 51543801856 | bytes 216008704 | tf_op jit(solution)/shard_map/dot_general | solution.py:13
  77.2 0.0 copy-start.1
  77.2 4.8 %fusion = f32[256]{0:T(256)S(1)} fusion(f32[256,8192]{1,0:T(8,128)} %get-tuple-element.6, f32[256]{0:T(256)S(1)} %get-tuple-element.5), kind=kLoop, calls=%fused_computation.4 | loop fusion | flops 4194048 | bytes 8390656 | tf_op jit(solution)/shard_map/reduce_sum | solution.py:17
  82.0 10.0 %all-gather.2 = f32[4,2,256]{2,1,0:T(2,128)S(1)} all-gather(f32[1,2,256]{2,1,0:T(2,128)S(1)} %maximum_bitcast_fusion), channel_id=2, replica_groups=mesh['dp'=2,'vp'=4] {'vp'}, dimensions={0}, use_global_device_ids=true | all-gather | bytes 10240 | tf_op jit(solution)/shard_map/all_gather | solution.py:18
  92.1 0.0 copy-done.1
  92.1 1.9 multiply_bitcast_fusion
  94.0 5.0 %copy.25 = f32[32,8,64,128]{3,2,1,0:T(8,128)} copy(f32[32,8,64,128]{3,1,2,0:T(8,128)S(1)} %multiply_bitcast_fusion) | data formatting | bytes 16777216
  99.0 9.2 %copy.18 = f32[256,64,128]{0,1,2:T(8,128)} copy(f32[256,64,128]{2,1,0:T(8,128)} %bitcast.35) | data formatting | bytes 16777216 | tf_op jit(solution)/shard_map/reshape.2
  108.2 7.4 %fusion.8 = f32[256,64,128]{0,1,2:T(8,128)} fusion(f32[256,64,128]{0,1,2:T(8,128)} %copy.18), kind=kOutput, calls=%fused_computation.29 | output fusion | flops 266338304 | bytes 16777216 | tf_op jit(solution)/shard_map/reduce-window
  115.6 0.8 slice_bitcast_fusion
  116.4 0.1 reduce-window.9
  116.6 4.2 %broadcast_add_fusion.2 = f32[256,64,128]{0,1,2:T(8,128)S(1)} fusion(f32[256,64,128]{0,1,2:T(8,128)} %fusion.8, f32[256,64]{0,1:T(8,128)S(1)} %slice.26), kind=kLoop, calls=%fused_computation.7 | loop fusion | flops 2097152 | bytes 16842752 | tf_op jit(solution)/shard_map/reduce_window_sum
  120.8 0.0 copy-start
  120.8 3.4 %copy-done = f32[256,64,128]{0,1,2:T(8,128)} copy-done((f32[256,64,128]{0,1,2:T(8,128)}, f32[256,64,128]{0,1,2:T(8,128)S(1)}, u32[]{:S(2)}) %copy-start) | copy-done | bytes 8388632
  124.2 8.1 %copy.20 = f32[256,64,128]{0,2,1:T(8,128)} copy(f32[256,64,128]{0,1,2:T(8,128)S(1)} %broadcast_add_fusion.2) | data formatting | bytes 16777216 | tf_op jit(solution)/shard_map/reduce_window_sum
  132.3 8.9 %copy.19 = f32[256,64,128]{2,1,0:T(8,128)} copy(f32[256,64,128]{0,1,2:T(8,128)} %copy-done) | data formatting | bytes 16777216 | tf_op jit(solution)/shard_map/reduce_window_sum
  141.2 0.7 slice.27
  141.9 6.7 %all-gather.1 = f32[1024,1]{0,1:T(1,128)S(1)} all-gather(f32[256,1]{0,1:T(1,128)S(1)} %slice.27), channel_id=3, replica_groups=mesh['dp'=2,'vp'=4] {'vp'}, dimensions={0}, use_global_device_ids=true | all-gather | bytes 5120 | tf_op jit(solution)/shard_map/all_gather | solution.py:23
  148.5 0.5 broadcast.50
  149.0 0.7 reduce.4
  149.7 9.4 %reduce_window_sum.20 = f32[4,64,8192]{2,1,0:T(8,128)} reshape(f32[256,64,128]{2,1,0:T(8,128)} %copy.19) | data formatting | bytes 16777216 | tf_op jit(solution)/shard_map/reduce_window_sum
  159.1 0.1 select_reduce_fusion
  159.2 0.1 add.24
  159.3 7.9 %broadcast_add_fusion.1 = f32[4,64,8192]{2,1,0:T(8,128)} fusion(f32[4,64,8192]{2,1,0:T(8,128)} %reduce_window_sum.20, f32[4,64]{1,0:T(4,128)S(1)} %add.24), kind=kLoop, calls=%fused_computation.6 | loop fusion | flops 2097152 | bytes 16778240 | tf_op jit(solution)/shard_map/add | solution.py:26
  167.2 0.0 copy-start.2
  167.2 5.8 %all-to-all-start = ((f32[4,64,8192]{2,1,0:T(8,128)}), f32[4,64,8192]{2,1,0:T(8,128)}, u32[]{:S(2)}, u32[]{:S(2)}) async-start(f32[4,64,8192]{2,1,0:T(8,128)} %broadcast_add_fusion.1), calls=%async_computation | async-start | bytes 16777216 | tf_op jit(solution)/shard_map/all_to_all | solution.py:31
  173.0 0.0 copy-done.2
  173.1 7.1 %broadcast_add_fusion = f32[256,8192]{0,1:T(8,128)} fusion(f32[256]{0:T(256)S(1)} %select_reduce_fusion, f32[256,64,128]{0,2,1:T(8,128)} %copy.20), kind=kLoop, calls=%fused_computation.5 | loop fusion | flops 2097152 | bytes 16778240 | tf_op jit(solution)/shard_map/add | solution.py:26
  180.2 7.7 %gather_fusion = f32[256]{0:T(256)S(1)} fusion(f32[256,8192]{0,1:T(8,128)} %broadcast_add_fusion, s32[256]{0:T(256)S(1)} %bitcast.36), kind=kCustom, calls=%fused_computation | custom fusion | bytes 4096 | tf_op jit(solution)/shard_map/jit(take_along_axis)/gather | solution.py:29
  188.0 80.0 %psum.7 = f32[256]{0:T(256)} all-reduce(f32[256]{0:T(256)S(1)} %and_select_fusion.1), channel_id=1, replica_groups=mesh['dp'=2,'vp'=4] {'vp'}, use_global_device_ids=true, to_apply=%region_7.8 | all-reduce | flops 256 | bytes 2048 | tf_op jit(solution)/shard_map/psum | solution.py:30
  268.0 0.0 all-to-all-done
  268.0 7.7 %copy.24 = f32[4,8,8,8192]{3,2,0,1:T(8,128)} copy(f32[4,8,8,8192]{3,2,1,0:T(8,128)} %bitcast.11) | data formatting | bytes 16777216 | tf_op jit(solution)/shard_map/all_to_all | solution.py:31
  (12 shorter events, 0.1 us)
Async XLA Ops:
  77.2 14.9 %copy-start.1 = (f32[256,8192]{1,0:T(8,128)S(1)}, f32[256,8192]{1,0:T(8,128)}, u32[]{:S(2)}) copy-start(f32[256,8192]{1,0:T(8,128)} %get-tuple-element.6) | copy-start | bytes 25165828
  120.8 3.4 %copy-start = (f32[256,64,128]{0,1,2:T(8,128)}, f32[256,64,128]{0,1,2:T(8,128)S(1)}, u32[]{:S(2)}) copy-start(f32[256,64,128]{0,1,2:T(8,128)S(1)} %broadcast_add_fusion.2) | copy-start | bytes 25165828
  167.2 5.8 %copy-start.2 = (s32[256]{0:T(256)S(1)}, s32[256]{0:T(256)}, u32[]{:S(2)}) copy-start(s32[256]{0:T(256)} %param.7) | copy-start | bytes 3076
  167.2 100.8 %all-to-all-start = ((f32[4,64,8192]{2,1,0:T(8,128)}), f32[4,64,8192]{2,1,0:T(8,128)}, u32[]{:S(2)}, u32[]{:S(2)}) async-start(f32[4,64,8192]{2,1,0:T(8,128)} %broadcast_add_fusion.1), calls=%async_computation | async-start | bytes 16777216 | tf_op jit(solution)/shard_map/all_to_all | solution.py:31
where the time goes:
time: 277 us; the launch traced here: 276 us
  blocking collectives  96.7 us (35%)
  matrix products  76.6 us (28%)
  local copies, waits for them, and re-layouts  61.5 us (22%)
  other arithmetic  34.3 us (12%)
  starting transfers between devices  5.83 us (2%)
    psum x1, blocking collectives, local_step(): cdf_at_target = lax.psum(jnp.where(in_shard, picked, 0.0), 'vp')  80 us
    dot_general x1, matrix products, local_step(): logits = jnp.dot(hidden, w_local, preferred_element_type=jnp.float32)  76.6 us
    another operation x6, local copies, waits for them, and re-layouts  36.4 us
    add x2, other arithmetic, local_step(): cdf_cols = local_cdf + offset[:, None]  15.1 us
    another operation x3, other arithmetic  11.7 us
    all_gather x1, blocking collectives, local_step(): shard_stats = lax.all_gather(jnp.stack([local_max, local_sum]), 'vp')  9.99 us
    unnamed x8, local copies, waits for them, and re-layouts  8.43 us
    gather x1, local copies, waits for them, and re-layouts, local_step(): jnp.take_along_axis(cdf_cols, jnp.clip(local_ids, 0, local_vocab - 1)[:,...  7.71 us
  transfers between devices with their start and end apart: 1, of which 0 were waited for; matrix products, arithmetic and copies ran while one was open for 5% of the time, Pallas kernels for 0%

commit v1 on v0

v1 whole, which is shorter than its diff:
```python
import functools
import jax
import jax.numpy as jnp
from jax import lax
from jax.experimental import pallas as pl
from jax.experimental.pallas import tpu as pltpu
from jax.sharding import PartitionSpec as P

TILE = 256
K_CHUNK = 3072
PACE = (3, 4)
GROUP = 4
MESH = pl.DeviceIdType.MESH


def head_kernel(
    n_vp, rows, n_tiles, n_k,
    h_hbm, w_hbm, temp_ref, tgt_ref,
    tab_ref, cdf_ref,
    h_buf, w_buf, stage, acc, temp_b, tgt_b, m_l, s_l, g_l, st_out, st_in, col_b, tri,
    h_sem, w_sem, send_sem, recv_sem, st_send, st_recv,
):
    dp = lax.axis_index("dp")
    me = lax.axis_index("vp")
    batch = n_vp * rows
    local_vocab = n_tiles * TILE
    chip = me // 2
    mate = chip * 2 + lax.rem(me + 1, 2)
    far0 = (1 - chip) * 2 + lax.rem(me, 2)
    far1 = (1 - chip) * 2 + lax.rem(me + 1, 2)

    barrier = pltpu.get_barrier_semaphore()
    for peer in (mate, far0, far1):
        pl.semaphore_signal(barrier, inc=1, device_id=(dp, peer), device_id_type=MESH)

    def w_copy(t, kc):
        slot = lax.rem(t, 2) * n_k + kc
        return pltpu.make_async_copy(
            w_hbm.at[pl.ds(kc * K_CHUNK, K_CHUNK), pl.ds(pl.multiple_of(t * TILE, TILE), TILE)],
            w_buf.at[slot], w_sem.at[slot])

    def h_copy(kc):
        return pltpu.make_async_copy(
            h_hbm.at[:, pl.ds(kc * K_CHUNK, K_CHUNK)], h_buf.at[:, pl.ds(kc * K_CHUNK, K_CHUNK)], h_sem.at[kc])

    for kc in range(n_k):
        w_copy(0, kc).start()
        h_copy(kc).start()
    for kc in range(n_k):
        w_copy(1, kc).start()

    temp_b[...] = jnp.broadcast_to(temp_ref[...], (128, batch)).T
    tgt_b[...] = jnp.broadcast_to(tgt_ref[...].astype(jnp.float32), (128, batch)).T
    m_l[...] = jnp.full_like(m_l, -jnp.inf)
    s_l[...] = jnp.zeros_like(s_l)
    g_l[...] = jnp.zeros_like(g_l)
    r_id = lax.broadcasted_iota(jnp.int32, (TILE, TILE), 0)
    c_id = lax.broadcasted_iota(jnp.int32, (TILE, TILE), 1)
    upper = jnp.where(r_id <= c_id, 1.0, 0.0).astype(jnp.bfloat16)
    for q in range(3):
        tri[q * TILE:(q + 1) * TILE, :] = upper

    def send(t, peer, k):
        return pltpu.make_async_remote_copy(
            src_ref=stage.at[t, pl.ds(pl.multiple_of(peer * rows, rows), rows), :],
            dst_ref=tab_ref.at[:, pl.ds(pl.multiple_of(me * local_vocab + t * TILE, TILE), TILE)],
            send_sem=send_sem.at[k, t],
            recv_sem=recv_sem.at[me, t],
            device_id=(dp, peer), device_id_type=MESH)

    def recv(t, src):
        cols = tab_ref.at[:, pl.ds(pl.multiple_of(src * local_vocab + t * TILE, TILE), TILE)]
        return pltpu.make_async_remote_copy(
            src_ref=cols, dst_ref=cols, send_sem=send_sem.at[0, t], recv_sem=recv_sem.at[src, t],
            device_id=(dp, src), device_id_type=MESH)

    def send_far(t):
        send(t, far0, 1).start()
        send(t, far1, 2).start()

    def tile(t, first):
        for kc in range(n_k):
            if first:
                h_copy(kc).wait()
            w_copy(t, kc).wait()
            slot = lax.rem(t, 2) * n_k + kc
            part = jnp.dot(h_buf[:, kc * K_CHUNK:(kc + 1) * K_CHUNK], w_buf[slot],
                           preferred_element_type=jnp.float32)
            if kc == 0:
                acc[...] = part
            elif kc < n_k - 1:
                acc[...] += part
            else:
                total = acc[...] + part

            if first:
                w_copy(t + 2, kc).start()
            else:
                @pl.when(t + 2 < n_tiles)
                def _():
                    w_copy(t + 2, kc).start()
        temp = temp_b[...]
        z0 = total[:, :128] * temp
        z1 = total[:, 128:] * temp
        stage[t, :, :128] = z0
        stage[t, :, 128:] = z1
        m_old = m_l[...]
        m_new = jnp.maximum(m_old, jnp.maximum(z0, z1))
        keep = jnp.exp(m_old - m_new)
        e0 = jnp.exp(z0 - m_new)
        e1 = jnp.exp(z1 - m_new)
        base = (me * local_vocab + t * TILE).astype(jnp.float32)
        dist = tgt_b[...] - base
        lane = lax.broadcasted_iota(jnp.int32, (batch, 128), 1).astype(jnp.float32)
        m_l[...] = m_new
        s_l[...] = s_l[...] * keep + (e0 + e1)
        g_l[...] = g_l[...] * keep + (jnp.where(lane <= dist, e0, 0.0) + jnp.where(lane + 128.0 <= dist, e1, 0.0))

    tile(jnp.int32(0), True)
    pl.semaphore_wait(barrier, n_vp - 1)
    send_far(0)
    send(0, mate, 0).start()

    num, den = PACE

    def step(t, carry):
        tile(t, False)
        now, before = (t * num) // den, ((t - 1) * num) // den

        @pl.when(now > before)
        def _():
            send_far(now)
        send(t, mate, 0).start()
        return carry

    lax.fori_loop(1, n_tiles, step, 0)

    m_lane = m_l[...]
    m_dev = jnp.max(m_lane, axis=1, keepdims=True)
    w_lane = jnp.exp(m_lane - m_dev)
    s_dev = jnp.sum(s_l[...] * w_lane, axis=1, keepdims=True)
    g_dev = jnp.sum(g_l[...] * w_lane, axis=1, keepdims=True)
    lane = lax.broadcasted_iota(jnp.int32, (batch, 128), 1)
    packed = jnp.where(lane == 0, m_dev, jnp.where(lane == 1, s_dev, jnp.where(lane == 2, g_dev, 0.0)))
    stats = packed.T[:8, :]
    st_out[...] = stats
    st_in[me] = stats

    def st_copy(peer, k):
        return pltpu.make_async_remote_copy(
            src_ref=st_out, dst_ref=st_in.at[me], send_sem=st_send.at[k], recv_sem=st_recv.at[me],
            device_id=(dp, peer), device_id_type=MESH)

    def st_wait(src):
        pltpu.make_async_remote_copy(
            src_ref=st_out, dst_ref=st_in.at[src], send_sem=st_send.at[0], recv_sem=st_recv.at[src],
            device_id=(dp, src), device_id_type=MESH).wait_recv()

    peers = ((far0, 1), (far1, 2), (mate, 0))
    for peer, k in peers:
        st_copy(peer, k).start()
    for t in range(((n_tiles - 1) * num) // den + 1, n_tiles):
        send_far(t)
    for peer, k in peers:
        st_wait(peer)

    everyone = [st_in[i] for i in range(n_vp)]
    m_all = functools.reduce(jnp.maximum, [x[0:1] for x in everyone])
    weight = [jnp.exp(x[0:1] - m_all) for x in everyone]
    s_w = [x[1:2] * w for x, w in zip(everyone, weight)]
    inv = 1.0 / functools.reduce(jnp.add, s_w)
    cdf_ref[...] = functools.reduce(jnp.add, [x[2:3] * w for x, w in zip(everyone, weight)]) * inv
    offsets, running = [], jnp.zeros_like(inv)
    for x in s_w:
        offsets.append(running * inv)
        running = running + x
    sub = lax.broadcasted_iota(jnp.int32, (128, batch), 0)
    table = jnp.zeros((128, batch), jnp.float32)
    for i, row in enumerate([m_all, inv] + offsets):
        table = jnp.where(sub == i, row, table)
    col_b[...] = table.T
    mine = col_b[pl.ds(pl.multiple_of(me * rows, rows), rows), :]
    m_col, inv_col = mine[:, 0:1], mine[:, 1:2]
    lane_r = lax.broadcasted_iota(jnp.int32, (rows, 128), 1)

    def offset(src):
        return jnp.sum(jnp.where(lane_r == src + 2, mine, 0.0), axis=1, keepdims=True)

    def finish(src, g, carry, own):
        parts = []
        for q in range(GROUP):
            t = g * GROUP + q
            if own:
                z = stage[t, pl.ds(pl.multiple_of(me * rows, rows), rows), :]
            else:
                recv(t, src).wait_recv()
                z = tab_ref[:, pl.ds(pl.multiple_of(src * local_vocab + t * TILE, TILE), TILE)]
            parts.append(jnp.exp(z - m_col) * inv_col)
        p = jnp.concatenate(parts, axis=0)
        hi = p.astype(jnp.bfloat16)
        rest = p - hi.astype(jnp.float32)
        mid = rest.astype(jnp.bfloat16)
        low = (rest - mid.astype(jnp.float32)).astype(jnp.bfloat16)
        c = jnp.dot(jnp.concatenate([hi, mid, low], axis=1), tri[...], preferred_element_type=jnp.float32)
        for q in range(GROUP):
            t = g * GROUP + q
            cq = c[q * rows:(q + 1) * rows, :]
            tab_ref[:, pl.ds(pl.multiple_of(src * local_vocab + t * TILE, TILE), TILE)] = cq + carry
            carry = carry + cq[:, TILE - 1:TILE]
        return carry

    n_groups = n_tiles // GROUP
    lax.fori_loop(0, n_groups, lambda g, c: finish(me, g, c, True), offset(me))
    lax.fori_loop(0, n_groups, lambda g, c: finish(mate, g, c, False), offset(mate))
    lax.fori_loop(0, n_groups, lambda g, c: (finish(far0, g, c[0], False), finish(far1, g, c[1], False)),
                  (offset(far0), offset(far1)))

    def drain(t, carry):
        for peer, k in peers:
            send(t, peer, k).wait_send()
        return carry

    lax.fori_loop(0, n_tiles, drain, 0)
    for peer, k in peers:
        st_copy(peer, k).wait_send()


def solution(mesh):
    n_vp = mesh.shape["vp"]

    def local_step(hidden, w_local, inv_temp, target_ids):
        batch, depth = hidden.shape
        rows = batch // n_vp
        local_vocab = w_local.shape[1]
        n_tiles, n_k = local_vocab // TILE, depth // K_CHUNK
        f32 = jnp.float32
        vmem = pl.BlockSpec(memory_space=pltpu.VMEM)
        hbm = pl.BlockSpec(memory_space=pl.ANY)
        table, at_target = pl.pallas_call(
            functools.partial(head_kernel, n_vp, rows, n_tiles, n_k),
            out_shape=(pltpu.VMEM((rows, n_vp * local_vocab), f32),
                       jax.ShapeDtypeStruct((1, batch), f32)),
            in_specs=[hbm, hbm, vmem, vmem],
            out_specs=(vmem, vmem),
            scratch_shapes=[
                pltpu.VMEM((batch, depth), jnp.bfloat16),
                pltpu.VMEM((2 * n_k, K_CHUNK, TILE), jnp.bfloat16),
                pltpu.VMEM((n_tiles, batch, TILE), f32),
                pltpu.VMEM((batch, TILE), f32),
                pltpu.VMEM((batch, 128), f32),
                pltpu.VMEM((batch, 128), f32),
                pltpu.VMEM((batch, 128), f32),
                pltpu.VMEM((batch, 128), f32),
                pltpu.VMEM((batch, 128), f32),
                pltpu.VMEM((8, batch), f32),
                pltpu.VMEM((n_vp, 8, batch), f32),
                pltpu.VMEM((batch, 128), f32),
                pltpu.VMEM((3 * TILE, TILE), jnp.bfloat16),
                pltpu.SemaphoreType.DMA((n_k,)),
                pltpu.SemaphoreType.DMA((2 * n_k,)),
                pltpu.SemaphoreType.DMA((3, n_tiles)),
                pltpu.SemaphoreType.DMA((n_vp, n_tiles)),
                pltpu.SemaphoreType.DMA((3,)),
                pltpu.SemaphoreType.DMA((n_vp,)),
            ],
            compiler_params=pltpu.CompilerParams(
                collective_id=0, has_side_effects=True, vmem_limit_bytes=38 * 2**20),
        )(hidden, w_local, inv_temp[None, :], target_ids[None, :])
        return table, at_target[0]

    return jax.shard_map(
        local_step,
        mesh=mesh,
        in_specs=(P("dp", None), P(None, "vp"), P("dp"), P("dp")),
        out_specs=(P(("dp", "vp"), None), P("dp")),
        check_vma=False,
    )
```

time: 277 us -> 164 us (0.59)
  Pallas kernels: 0 us -> 155 us
  blocking collectives: 96.7 us -> 0 us
  matrix products: 76.6 us -> 0 us
  local copies, waits for them, and re-layouts: 61.5 us -> 8.1 us
  other arithmetic: 34.3 us -> 0 us
  starting transfers between devices: 5.83 us -> 0 us
    pallas_call x0 -> x1, Pallas kernels: none -> 155 us  [local_step(): pl.pallas_call(functools.partial(head_kernel, n_vp, rows, n_tiles, n_k),...]
    psum x1 -> x0, blocking collectives: 80 us -> none  [local_step(): cdf_at_target = lax.psum(jnp.where(in_shard, picked, 0.0), 'vp')]
    dot_general x1 -> x0, matrix products: 76.6 us -> none  [local_step(): logits = jnp.dot(hidden, w_local, preferred_element_type=jnp.float32)]
    another operation x6 -> x0, local copies, waits for them, and re-layouts: 36.4 us -> none
    all_gather x2 -> x0, blocking collectives: 16.7 us -> none  [the longest x1 9.99 us: local_step(): shard_stats = lax.all_gather(jnp.stack([local_max, local_sum]), 'vp')]
    add x2 -> x0, other arithmetic: 15.1 us -> none  [local_step(): cdf_cols = local_cdf + offset[:, None]]
    another operation x3 -> x0, other arithmetic: 11.7 us -> none
    gather x1 -> x0, local copies, waits for them, and re-layouts: 7.71 us -> none  [local_step(): jnp.take_along_axis(cdf_cols, jnp.clip(local_ids, 0, local_vocab - 1)[:,...]
  transfers between devices with their start and end apart: 1 -> 0, of which waited for: 0 -> 0; matrix products, arithmetic and copies ran while one was open for 5% -> 0% of each run, Pallas kernels for 0% -> 0%
where the time goes in v1:
time: 164 us
  Pallas kernels  155 us (95%)
  local copies, waits for them, and re-layouts  8.1 us (5%)
    pallas_call x1, Pallas kernels, local_step(): pl.pallas_call(functools.partial(head_kernel, n_vp, rows, n_tiles, n_k),...  155 us
    unnamed x8, local copies, waits for them, and re-layouts  8.1 us

profile of v1, /device:TPU:0, one launch (start us, length us, event | category | flops | bytes accessed | tf_op | source)
XLA Modules:
  0.0 163.8 jit_solution(12834175798942086354)
XLA Ops:
  0.6 0.0 copy-start
  0.6 2.8 %copy-done = bf16[256,12288]{1,0:T(8,128)(2,1)S(1)} copy-done((bf16[256,12288]{1,0:T(8,128)(2,1)S(1)}, bf16[256,12288]{1,0:T(8,128)(2,1)}, u32[]{:S(2)}) %copy-start) | copy-done | bytes 6291480
  3.4 0.0 copy-start.1
  3.4 0.7 copy-done.1
  4.1 0.0 copy-start.2
  4.1 0.7 copy-done.2
  4.8 155.0 %shard_map.59 = (f32[64,32768]{1,0:T(8,128)S(1)}, f32[1,256]{1,0:T(1,128)S(1)}) custom-call(bf16[256,12288]{1,0:T(8,128)(2,1)S(1)} %copy-done, bf16[12288,8192]{1,0:T(8,128)(2,1)} %w_hbm.1, f32[1,256]{1,0:T(1,128)S(1)} %bitcast.4, s32[1,256]{1,0:T(1,128)S(1)} %bitcast.5), custom_call_target="tpu_custom_call" | custom-call | tf_op jit(solution)/shard_map/pallas_call | solution.py:239
  159.8 3.4 %copy.8 = f32[64,32768]{1,0:T(8,128)} copy(f32[64,32768]{1,0:T(8,128)S(1)} %get-tuple-element.6) | data formatting | bytes 16777216
  163.2 0.6 copy.9
Async XLA Ops:
  0.6 2.8 %copy-start = (bf16[256,12288]{1,0:T(8,128)(2,1)S(1)}, bf16[256,12288]{1,0:T(8,128)(2,1)}, u32[]{:S(2)}) copy-start(bf16[256,12288]{1,0:T(8,128)(2,1)} %h_hbm.1) | copy-start | bytes 18874372
  3.4 0.7 copy-start.1
  4.1 0.7 copy-start.2

commit v2 on v1

--- a/solution.py
+++ b/solution.py
@@ -7,18 +7,19 @@
 from jax.sharding import PartitionSpec as P
 
 TILE = 256
-K_CHUNK = 3072
+SLOTS = 3
+PIECES = 4
 PACE = (3, 4)
 GROUP = 4
 MESH = pl.DeviceIdType.MESH
 
 
 def head_kernel(
-    n_vp, rows, n_tiles, n_k,
+    n_vp, rows, n_tiles,
     h_hbm, w_hbm, temp_ref, tgt_ref,
     tab_ref, cdf_ref,
-    h_buf, w_buf, stage, acc, temp_b, tgt_b, m_l, s_l, g_l, st_out, st_in, col_b, tri,
-    h_sem, w_sem, send_sem, recv_sem, st_send, st_recv,
+    h_buf, w_buf, stage, temp_b, tgt_b, m_l, s_l, g_l, st_out, st_in, col_b, tri,
+    h_sem, w0_sem, w_sem, send_sem, recv_sem, st_send, st_recv,
 ):
     dp = lax.axis_index("dp")
     me = lax.axis_index("vp")
@@ -33,21 +34,24 @@
     for peer in (mate, far0, far1):
         pl.semaphore_signal(barrier, inc=1, device_id=(dp, peer), device_id_type=MESH)
 
-    def w_copy(t, kc):
-        slot = lax.rem(t, 2) * n_k + kc
+    depth = h_buf.shape[1]
+    piece = depth // PIECES
+
+    def w_copy(t):
+        slot = lax.rem(t, SLOTS)
         return pltpu.make_async_copy(
-            w_hbm.at[pl.ds(kc * K_CHUNK, K_CHUNK), pl.ds(pl.multiple_of(t * TILE, TILE), TILE)],
-            w_buf.at[slot], w_sem.at[slot])
-
-    def h_copy(kc):
-        return pltpu.make_async_copy(
-            h_hbm.at[:, pl.ds(kc * K_CHUNK, K_CHUNK)], h_buf.at[:, pl.ds(kc * K_CHUNK, K_CHUNK)], h_sem.at[kc])
-
-    for kc in range(n_k):
-        w_copy(0, kc).start()
-        h_copy(kc).start()
-    for kc in range(n_k):
-        w_copy(1, kc).start()
+            w_hbm.at[:, pl.ds(pl.multiple_of(t * TILE, TILE), TILE)], w_buf.at[slot], w_sem.at[slot])
+
+    def first_copies(i):
+        span = pl.ds(i * piece, piece)
+        return (pltpu.make_async_copy(w_hbm.at[span, pl.ds(0, TILE)], w_buf.at[0, span, :], w0_sem.at[i]),
+                pltpu.make_async_copy(h_hbm.at[:, span], h_buf.at[:, span], h_sem.at[i]))
+
+    for i in range(PIECES):
+        for copy in first_copies(i):
+            copy.start()
+    for t in range(1, SLOTS):
+        w_copy(jnp.int32(t)).start()
 
     temp_b[...] = jnp.broadcast_to(temp_ref[...], (128, batch)).T
     tgt_b[...] = jnp.broadcast_to(tgt_ref[...].astype(jnp.float32), (128, batch)).T
@@ -79,26 +83,21 @@
         send(t, far1, 2).start()
 
     def tile(t, first):
-        for kc in range(n_k):
-            if first:
-                h_copy(kc).wait()
-            w_copy(t, kc).wait()
-            slot = lax.rem(t, 2) * n_k + kc
-            part = jnp.dot(h_buf[:, kc * K_CHUNK:(kc + 1) * K_CHUNK], w_buf[slot],
-                           preferred_element_type=jnp.float32)
-            if kc == 0:
-                acc[...] = part
-            elif kc < n_k - 1:
-                acc[...] += part
-            else:
-                total = acc[...] + part
-
-            if first:
-                w_copy(t + 2, kc).start()
-            else:
-                @pl.when(t + 2 < n_tiles)
-                def _():
-                    w_copy(t + 2, kc).start()
+        if first:
+            for i in range(PIECES):
+                for copy in first_copies(i):
+                    copy.wait()
+                part = jnp.dot(h_buf[:, i * piece:(i + 1) * piece], w_buf[0, i * piece:(i + 1) * piece, :],
+                               preferred_element_type=jnp.float32)
+                total = part if i == 0 else total + part
+            w_copy(t + SLOTS).start()
+        else:
+            w_copy(t).wait()
+            total = jnp.dot(h_buf[...], w_buf[lax.rem(t, SLOTS)], preferred_element_type=jnp.float32)
+
+            @pl.when(t + SLOTS < n_tiles)
+            def _():
+                w_copy(t + SLOTS).start()
         temp = temp_b[...]
         z0 = total[:, :128] * temp
         z1 = total[:, 128:] * temp
@@ -232,21 +231,20 @@
         batch, depth = hidden.shape
         rows = batch // n_vp
         local_vocab = w_local.shape[1]
-        n_tiles, n_k = local_vocab // TILE, depth // K_CHUNK
+        n_tiles = local_vocab // TILE
         f32 = jnp.float32
         vmem = pl.BlockSpec(memory_space=pltpu.VMEM)
         hbm = pl.BlockSpec(memory_space=pl.ANY)
         table, at_target = pl.pallas_call(
-            functools.partial(head_kernel, n_vp, rows, n_tiles, n_k),
+            functools.partial(head_kernel, n_vp, rows, n_tiles),
             out_shape=(pltpu.VMEM((rows, n_vp * local_vocab), f32),
                        jax.ShapeDtypeStruct((1, batch), f32)),
             in_specs=[hbm, hbm, vmem, vmem],
             out_specs=(vmem, vmem),
             scratch_shapes=[
                 pltpu.VMEM((batch, depth), jnp.bfloat16),
-                pltpu.VMEM((2 * n_k, K_CHUNK, TILE), jnp.bfloat16),
+                pltpu.VMEM((SLOTS, depth, TILE), jnp.bfloat16),
                 pltpu.VMEM((n_tiles, batch, TILE), f32),
-                pltpu.VMEM((batch, TILE), f32),
                 pltpu.VMEM((batch, 128), f32),
                 pltpu.VMEM((batch, 128), f32),
                 pltpu.VMEM((batch, 128), f32),
@@ -256,15 +254,16 @@
                 pltpu.VMEM((n_vp, 8, batch), f32),
                 pltpu.VMEM((batch, 128), f32),
                 pltpu.VMEM((3 * TILE, TILE), jnp.bfloat16),
-                pltpu.SemaphoreType.DMA((n_k,)),
-                pltpu.SemaphoreType.DMA((2 * n_k,)),
+                pltpu.SemaphoreType.DMA((PIECES,)),
+                pltpu.SemaphoreType.DMA((PIECES,)),
+                pltpu.SemaphoreType.DMA((SLOTS,)),
                 pltpu.SemaphoreType.DMA((3, n_tiles)),
                 pltpu.SemaphoreType.DMA((n_vp, n_tiles)),
                 pltpu.SemaphoreType.DMA((3,)),
                 pltpu.SemaphoreType.DMA((n_vp,)),
             ],
             compiler_params=pltpu.CompilerParams(
-                collective_id=0, has_side_effects=True, vmem_limit_bytes=38 * 2**20),
+                collective_id=0, has_side_effects=True, vmem_limit_bytes=45 * 2**20),
         )(hidden, w_local, inv_temp[None, :], target_ids[None, :])
         return table, at_target[0]
 

time: 164 us -> 111 us (0.68)
  Pallas kernels: 155 us -> 105 us
  local copies, waits for them, and re-layouts: 8.1 us -> 5.31 us
    pallas_call x1, Pallas kernels: 155 us -> 105 us  [local_step(): pl.pallas_call(functools.partial(head_kernel, n_vp, rows, n_tiles), out_s...]
    unnamed x8 -> x6, local copies, waits for them, and re-layouts: 8.1 us -> 5.31 us
where the time goes in v2:
time: 111 us
  Pallas kernels  105 us (95%)
  local copies, waits for them, and re-layouts  5.31 us (5%)
    pallas_call x1, Pallas kernels, local_step(): pl.pallas_call(functools.partial(head_kernel, n_vp, rows, n_tiles), out_s...  105 us
    unnamed x6, local copies, waits for them, and re-layouts  5.31 us

profile of v2, /device:TPU:0, one launch (start us, length us, event | category | flops | bytes accessed | tf_op | source)
XLA Modules:
  0.0 111.3 jit_solution(9697311887341783934)
XLA Ops:
  0.6 0.0 copy-start
  0.6 0.7 copy-done
  1.3 0.0 copy-start.1
  1.3 0.7 copy-done.1
  2.0 105.3 %shard_map.59 = (f32[64,32768]{1,0:T(8,128)S(1)}, f32[1,256]{1,0:T(1,128)S(1)}) custom-call(bf16[256,12288]{1,0:T(8,128)(2,1)} %h_hbm.1, bf16[12288,8192]{1,0:T(8,128)(2,1)} %w_hbm.1, f32[1,256]{1,0:T(1,128)S(1)} %bitcast.4, s32[1,256]{1,0:T(1,128)S(1)} %bitcast.5), custom_call_target="tpu_custom_call" | custom-call | tf_op jit(solution)/shard_map/pallas_call | solution.py:238
  107.3 3.4 %copy.8 = f32[64,32768]{1,0:T(8,128)} copy(f32[64,32768]{1,0:T(8,128)S(1)} %get-tuple-element.6) | data formatting | bytes 16777216
  110.7 0.6 copy.9
Async XLA Ops:
  0.6 0.7 copy-start
  1.3 0.7 copy-start.1

commit v3 on v2

--- a/solution.py
+++ b/solution.py
@@ -9,17 +9,17 @@
 TILE = 256
 SLOTS = 3
 PIECES = 4
-PACE = (3, 4)
+PACE = (3, 6, 4)
 GROUP = 4
 MESH = pl.DeviceIdType.MESH
 
 
 def head_kernel(
     n_vp, rows, n_tiles,
-    h_hbm, w_hbm, temp_ref, tgt_ref,
+    h_hbm, w_hbm, temp_hbm, tgt_hbm,
     tab_ref, cdf_ref,
-    h_buf, w_buf, stage, temp_b, tgt_b, m_l, s_l, g_l, st_out, st_in, col_b, tri,
-    h_sem, w0_sem, w_sem, send_sem, recv_sem, st_send, st_recv,
+    h_buf, w_buf, temp_ref, tgt_ref, stage, temp_b, tgt_b, m_l, s_l, g_l, st_out, st_in, col_b, tri,
+    in_sem, h_sem, w0_sem, w_sem, half_send, half_recv, send_sem, recv_sem, st_send, st_recv,
 ):
     dp = lax.axis_index("dp")
     me = lax.axis_index("vp")
@@ -42,16 +42,33 @@
         return pltpu.make_async_copy(
             w_hbm.at[:, pl.ds(pl.multiple_of(t * TILE, TILE), TILE)], w_buf.at[slot], w_sem.at[slot])
 
-    def first_copies(i):
+    near = pl.multiple_of(chip * 2 * rows, 2 * rows)
+    far = pl.multiple_of((1 - chip) * 2 * rows, 2 * rows)
+
+    def h_copy(part, i):
         span = pl.ds(i * piece, piece)
-        return (pltpu.make_async_copy(w_hbm.at[span, pl.ds(0, TILE)], w_buf.at[0, span, :], w0_sem.at[i]),
-                pltpu.make_async_copy(h_hbm.at[:, span], h_buf.at[:, span], h_sem.at[i]))
+        block = pl.ds(far if part == 0 else near, 2 * rows)
+        return pltpu.make_async_copy(h_hbm.at[block, span], h_buf.at[block, span], h_sem.at[part, i])
+
+    def w_half(part, i):
+        span, cols = pl.ds(i * piece, piece), pl.ds(part * 128, 128)
+        return pltpu.make_async_copy(w_hbm.at[span, cols], w_buf.at[0, span, cols], w0_sem.at[part, i])
 
     for i in range(PIECES):
-        for copy in first_copies(i):
-            copy.start()
+        w_half(0, i).start()
+        h_copy(0, i).start()
+    small = (pltpu.make_async_copy(temp_hbm, temp_ref, in_sem.at[0]),
+             pltpu.make_async_copy(tgt_hbm, tgt_ref, in_sem.at[1]))
+    for copy in small:
+        copy.start()
+    for i in range(PIECES):
+        w_half(1, i).start()
+    for i in range(PIECES):
+        h_copy(1, i).start()
     for t in range(1, SLOTS):
         w_copy(jnp.int32(t)).start()
+    for copy in small:
+        copy.wait()
 
     temp_b[...] = jnp.broadcast_to(temp_ref[...], (128, batch)).T
     tgt_b[...] = jnp.broadcast_to(tgt_ref[...].astype(jnp.float32), (128, batch)).T
@@ -82,27 +99,61 @@
         send(t, far0, 1).start()
         send(t, far1, 2).start()
 
-    def tile(t, first):
-        if first:
-            for i in range(PIECES):
-                for copy in first_copies(i):
-                    copy.wait()
-                part = jnp.dot(h_buf[:, i * piece:(i + 1) * piece], w_buf[0, i * piece:(i + 1) * piece, :],
-                               preferred_element_type=jnp.float32)
-                total = part if i == 0 else total + part
+    def half(block, cols, part, wait_h):
+        total = None
+        for i in range(PIECES):
+            w_half(part, i).wait()
+            if wait_h:
+                h_copy(0, i).wait()
+            x = jnp.dot(h_buf[pl.ds(block, 2 * rows), i * piece:(i + 1) * piece],
+                        w_buf[0, i * piece:(i + 1) * piece, cols], preferred_element_type=jnp.float32)
+            total = x if i == 0 else total + x
+        stage[0, pl.ds(block, 2 * rows), cols] = total * temp_b[pl.ds(block, 2 * rows), :]
+
+    def send_half(part):
+        cols = pl.ds(part * 128, 128)
+        return [pltpu.make_async_remote_copy(
+            src_ref=stage.at[0, pl.ds(pl.multiple_of(peer * rows, rows), rows), cols],
+            dst_ref=tab_ref.at[:, pl.ds(pl.multiple_of(me * local_vocab + part * 128, 128), 128)],
+            send_sem=half_send.at[k, part], recv_sem=half_recv.at[me, part],
+            device_id=(dp, peer), device_id_type=MESH) for k, peer in enumerate((far0, far1))]
+
+    def first_tile():
+        half(far, slice(0, 128), 0, True)
+        pl.semaphore_wait(barrier, n_vp - 1)
+        for copy in send_half(0):
+            copy.start()
+        half(far, slice(128, 256), 1, False)
+        total = None
+        for i in range(PIECES):
+            h_copy(1, i).wait()
+            x = jnp.dot(h_buf[pl.ds(near, 2 * rows), i * piece:(i + 1) * piece],
+                        w_buf[0, i * piece:(i + 1) * piece, :], preferred_element_type=jnp.float32)
+            total = x if i == 0 else total + x
+            if i == 0:
+                for copy in send_half(1):
+                    copy.start()
+        w_copy(jnp.int32(SLOTS)).start()
+        temp = temp_b[pl.ds(near, 2 * rows), :]
+        stage[0, pl.ds(near, 2 * rows), :128] = total[:, :128] * temp
+        stage[0, pl.ds(near, 2 * rows), 128:] = total[:, 128:] * temp
+        statistics(jnp.int32(0), stage[0, :, :128], stage[0, :, 128:])
+
+    def tile(t):
+        w_copy(t).wait()
+        total = jnp.dot(h_buf[...], w_buf[lax.rem(t, SLOTS)], preferred_element_type=jnp.float32)
+
+        @pl.when(t + SLOTS < n_tiles)
+        def _():
             w_copy(t + SLOTS).start()
-        else:
-            w_copy(t).wait()
-            total = jnp.dot(h_buf[...], w_buf[lax.rem(t, SLOTS)], preferred_element_type=jnp.float32)
-
-            @pl.when(t + SLOTS < n_tiles)
-            def _():
-                w_copy(t + SLOTS).start()
         temp = temp_b[...]
         z0 = total[:, :128] * temp
         z1 = total[:, 128:] * temp
         stage[t, :, :128] = z0
         stage[t, :, 128:] = z1
+        statistics(t, z0, z1)
+
+    def statistics(t, z0, z1):
         m_old = m_l[...]
         m_new = jnp.maximum(m_old, jnp.maximum(z0, z1))
         keep = jnp.exp(m_old - m_new)
@@ -115,18 +166,18 @@
         s_l[...] = s_l[...] * keep + (e0 + e1)
         g_l[...] = g_l[...] * keep + (jnp.where(lane <= dist, e0, 0.0) + jnp.where(lane + 128.0 <= dist, e1, 0.0))
 
-    tile(jnp.int32(0), True)
-    pl.semaphore_wait(barrier, n_vp - 1)
-    send_far(0)
+    first_tile()
     send(0, mate, 0).start()
-
-    num, den = PACE
+    num, lead, den = PACE
+
+    def started(t):
+        return jnp.minimum(t, (t * num + lead) // den)
 
     def step(t, carry):
-        tile(t, False)
-        now, before = (t * num) // den, ((t - 1) * num) // den
-
-        @pl.when(now > before)
+        tile(t)
+        now = started(t)
+
+        @pl.when(now > started(t - 1))
         def _():
             send_far(now)
         send(t, mate, 0).start()
@@ -158,7 +209,7 @@
     peers = ((far0, 1), (far1, 2), (mate, 0))
     for peer, k in peers:
         st_copy(peer, k).start()
-    for t in range(((n_tiles - 1) * num) // den + 1, n_tiles):
+    for t in range(min(n_tiles - 1, ((n_tiles - 1) * num + lead) // den) + 1, n_tiles):
         send_far(t)
     for peer, k in peers:
         st_wait(peer)
@@ -185,15 +236,15 @@
     def offset(src):
         return jnp.sum(jnp.where(lane_r == src + 2, mine, 0.0), axis=1, keepdims=True)
 
-    def finish(src, g, carry, own):
+    def finish(items, carries):
+        carries = dict(carries)
         parts = []
-        for q in range(GROUP):
-            t = g * GROUP + q
-            if own:
+        for kind, src, t in items:
+            cols = pl.ds(pl.multiple_of(src * local_vocab + t * TILE, TILE), TILE)
+            if kind == "own":
                 z = stage[t, pl.ds(pl.multiple_of(me * rows, rows), rows), :]
             else:
-                recv(t, src).wait_recv()
-                z = tab_ref[:, pl.ds(pl.multiple_of(src * local_vocab + t * TILE, TILE), TILE)]
+                z = tab_ref[:, cols]
             parts.append(jnp.exp(z - m_col) * inv_col)
         p = jnp.concatenate(parts, axis=0)
         hi = p.astype(jnp.bfloat16)
@@ -201,27 +252,78 @@
         mid = rest.astype(jnp.bfloat16)
         low = (rest - mid.astype(jnp.float32)).astype(jnp.bfloat16)
         c = jnp.dot(jnp.concatenate([hi, mid, low], axis=1), tri[...], preferred_element_type=jnp.float32)
-        for q in range(GROUP):
-            t = g * GROUP + q
+        for q, (kind, src, t) in enumerate(items):
+            cols = pl.ds(pl.multiple_of(src * local_vocab + t * TILE, TILE), TILE)
             cq = c[q * rows:(q + 1) * rows, :]
-            tab_ref[:, pl.ds(pl.multiple_of(src * local_vocab + t * TILE, TILE), TILE)] = cq + carry
-            carry = carry + cq[:, TILE - 1:TILE]
+            tab_ref[:, cols] = cq + carries[kind]
+            carries[kind] = carries[kind] + cq[:, TILE - 1:TILE]
+        return carries
+
+    def run(kind, src, g, carry):
+        items = [(kind, src, g * GROUP + q) for q in range(GROUP)]
+        if kind != "own":
+            for _, _, t in items:
+                recv(t, src).wait_recv()
+        return finish(items, {kind: carry})[kind]
+
+    n_groups = n_tiles // GROUP
+    lax.fori_loop(0, n_groups, lambda g, c: run("own", me, g, c), offset(me))
+    lax.fori_loop(0, n_groups, lambda g, c: run("mate", mate, g, c), offset(mate))
+
+    def far_group(g, c, first):
+        out = []
+        for kind, src, carry in (("far0", far0, c[0]), ("far1", far1, c[1])):
+            items = [(kind, src, g * GROUP + q) for q in range(GROUP)]
+            for q, (_, _, t) in enumerate(items):
+                if first and q == 0:
+                    for part in range(2):
+                        cols = tab_ref.at[:, pl.ds(pl.multiple_of(src * local_vocab + part * 128, 128), 128)]
+                        pltpu.make_async_remote_copy(
+                            src_ref=cols, dst_ref=cols, send_sem=half_send.at[0, part],
+                            recv_sem=half_recv.at[src, part], device_id=(dp, src), device_id_type=MESH).wait_recv()
+                else:
+                    recv(t, src).wait_recv()
+            out.append(finish(items, {kind: carry})[kind])
+        return tuple(out)
+
+    c = far_group(0, (offset(far0), offset(far1)), True)
+    c = lax.fori_loop(1, n_groups - 1, lambda g, c: far_group(g, c, False), c)
+
+    def drain(t, carry):
+        send(t, mate, 0).wait_send()
         return carry
 
-    n_groups = n_tiles // GROUP
-    lax.fori_loop(0, n_groups, lambda g, c: finish(me, g, c, True), offset(me))
-    lax.fori_loop(0, n_groups, lambda g, c: finish(mate, g, c, False), offset(mate))
-    lax.fori_loop(0, n_groups, lambda g, c: (finish(far0, g, c[0], False), finish(far1, g, c[1], False)),
-                  (offset(far0), offset(far1)))
-
-    def drain(t, carry):
-        for peer, k in peers:
-            send(t, peer, k).wait_send()
+    def drain_far(t, carry):
+        send(t, far0, 1).wait_send()
+        send(t, far1, 2).wait_send()
         return carry
 
+    late = n_tiles - GROUP
     lax.fori_loop(0, n_tiles, drain, 0)
+    lax.fori_loop(1, late, drain_far, 0)
+    for part in range(2):
+        for copy in send_half(part):
+            copy.wait_send()
     for peer, k in peers:
         st_copy(peer, k).wait_send()
+    carries = {"far0": c[0], "far1": c[1]}
+    for t in range(late, n_tiles):
+        for src in (far0, far1):
+            recv(t, src).wait_recv()
+        carries = finish([("far0", far0, t), ("far1", far1, t)], carries)
+    lax.fori_loop(late, n_tiles, drain_far, 0)
+
+
+def write_kernel(tab_ref, cdf_ref, tab_out, cdf_out, sem):
+    rows = tab_ref.shape[0]
+    blocks = rows // 8
+    copies = [pltpu.make_async_copy(tab_ref.at[pl.ds(i * 8, 8), :], tab_out.at[pl.ds(i * 8, 8), :], sem.at[i])
+              for i in range(blocks)]
+    copies.append(pltpu.make_async_copy(cdf_ref, cdf_out, sem.at[blocks]))
+    for copy in copies:
+        copy.start()
+    for copy in copies:
+        copy.wait()
 
 
 def solution(mesh):
@@ -238,12 +340,14 @@
         table, at_target = pl.pallas_call(
             functools.partial(head_kernel, n_vp, rows, n_tiles),
             out_shape=(pltpu.VMEM((rows, n_vp * local_vocab), f32),
-                       jax.ShapeDtypeStruct((1, batch), f32)),
-            in_specs=[hbm, hbm, vmem, vmem],
+                       pltpu.VMEM((1, batch), f32)),
+            in_specs=[hbm, hbm, hbm, hbm],
             out_specs=(vmem, vmem),
             scratch_shapes=[
                 pltpu.VMEM((batch, depth), jnp.bfloat16),
                 pltpu.VMEM((SLOTS, depth, TILE), jnp.bfloat16),
+                pltpu.VMEM((1, batch), f32),
+                pltpu.VMEM((1, batch), jnp.int32),
                 pltpu.VMEM((n_tiles, batch, TILE), f32),
                 pltpu.VMEM((batch, 128), f32),
                 pltpu.VMEM((batch, 128), f32),
@@ -254,17 +358,28 @@
                 pltpu.VMEM((n_vp, 8, batch), f32),
                 pltpu.VMEM((batch, 128), f32),
                 pltpu.VMEM((3 * TILE, TILE), jnp.bfloat16),
-                pltpu.SemaphoreType.DMA((PIECES,)),
-                pltpu.SemaphoreType.DMA((PIECES,)),
+                pltpu.SemaphoreType.DMA((2,)),
+                pltpu.SemaphoreType.DMA((2, PIECES)),
+                pltpu.SemaphoreType.DMA((2, PIECES)),
                 pltpu.SemaphoreType.DMA((SLOTS,)),
+                pltpu.SemaphoreType.DMA((2, 2)),
+                pltpu.SemaphoreType.DMA((n_vp, 2)),
                 pltpu.SemaphoreType.DMA((3, n_tiles)),
                 pltpu.SemaphoreType.DMA((n_vp, n_tiles)),
                 pltpu.SemaphoreType.DMA((3,)),
                 pltpu.SemaphoreType.DMA((n_vp,)),
             ],
             compiler_params=pltpu.CompilerParams(
-                collective_id=0, has_side_effects=True, vmem_limit_bytes=45 * 2**20),
+                collective_id=0, has_side_effects=True, vmem_limit_bytes=46 * 2**20),
         )(hidden, w_local, inv_temp[None, :], target_ids[None, :])
+        table, at_target = pl.pallas_call(
+            write_kernel,
+            out_shape=(jax.ShapeDtypeStruct(table.shape, f32), jax.ShapeDtypeStruct(at_target.shape, f32)),
+            in_specs=[vmem, vmem],
+            out_specs=(hbm, hbm),
+            scratch_shapes=[pltpu.SemaphoreType.DMA((rows // 8 + 1,))],
+            compiler_params=pltpu.CompilerParams(vmem_limit_bytes=45 * 2**20),
+        )(table, at_target)
         return table, at_target[0]
 
     return jax.shard_map(

time: 111 us -> 111 us (level)
  Pallas kernels: 105 us -> 111 us
  local copies, waits for them, and re-layouts: 5.31 us -> 0 us
    unnamed x6 -> x0, local copies, waits for them, and re-layouts: 5.31 us -> none
    pallas_call x0 -> x1, Pallas kernels: none -> 3.38 us  [local_step(): pl.pallas_call(write_kernel, out_shape=(jax.ShapeDtypeStruct(table.shape,...]
    pallas_call x1, Pallas kernels: 105 us -> 107 us  [local_step(): pl.pallas_call(functools.partial(head_kernel, n_vp, rows, n_tiles), out_s...]
where the time goes in v3:
time: 111 us
  Pallas kernels  111 us (100%)
    pallas_call x1, Pallas kernels, local_step(): pl.pallas_call(functools.partial(head_kernel, n_vp, rows, n_tiles), out_s...  107 us
    pallas_call x1, Pallas kernels, local_step(): pl.pallas_call(write_kernel, out_shape=(jax.ShapeDtypeStruct(table.shape,...  3.38 us

profile of v3, /device:TPU:0, one launch (start us, length us, event | category | flops | bytes accessed | tf_op | source)
XLA Modules:
  0.0 111.3 jit_solution(6691569298397485753)
XLA Ops:
  0.6 107.3 %shard_map.59 = (f32[64,32768]{1,0:T(8,128)S(1)}, f32[1,256]{1,0:T(1,128)S(1)}) custom-call(bf16[256,12288]{1,0:T(8,128)(2,1)} %h_hbm.1, bf16[12288,8192]{1,0:T(8,128)(2,1)} %w_hbm.1, f32[1,256]{1,0:T(1,128)} %bitcast.3, s32[1,256]{1,0:T(1,128)} %bitcast.4), custom_call_target="tpu_custom_call" | custom-call | tf_op jit(solution)/shard_map/pallas_call | solution.py:340
  107.9 3.4 %shard_map.60 = (f32[64,32768]{1,0:T(8,128)}, f32[1,256]{1,0:T(1,128)}) custom-call(f32[64,32768]{1,0:T(8,128)S(1)} %get-tuple-element.6.tab_ref, f32[1,256]{1,0:T(1,128)S(1)} %get-tuple-element.7.cdf_ref), custom_call_target="tpu_custom_call" | custom-call | tf_op jit(solution)/shard_map/pallas_call | solution.py:375

commit v4 on v3

--- a/solution.py
+++ b/solution.py
@@ -54,19 +54,19 @@
         span, cols = pl.ds(i * piece, piece), pl.ds(part * 128, 128)
         return pltpu.make_async_copy(w_hbm.at[span, cols], w_buf.at[0, span, cols], w0_sem.at[part, i])
 
-    for i in range(PIECES):
-        w_half(0, i).start()
-        h_copy(0, i).start()
     small = (pltpu.make_async_copy(temp_hbm, temp_ref, in_sem.at[0]),
              pltpu.make_async_copy(tgt_hbm, tgt_ref, in_sem.at[1]))
     for copy in small:
         copy.start()
     for i in range(PIECES):
-        w_half(1, i).start()
+        w_half(0, i).start(priority=1)
+        h_copy(0, i).start(priority=1)
     for i in range(PIECES):
-        h_copy(1, i).start()
+        w_half(1, i).start(priority=1)
+    for i in range(PIECES):
+        h_copy(1, i).start(priority=1)
     for t in range(1, SLOTS):
-        w_copy(jnp.int32(t)).start()
+        w_copy(jnp.int32(t)).start(priority=1)
     for copy in small:
         copy.wait()
 
@@ -133,7 +133,7 @@
             if i == 0:
                 for copy in send_half(1):
                     copy.start()
-        w_copy(jnp.int32(SLOTS)).start()
+        w_copy(jnp.int32(SLOTS)).start(priority=1)
         temp = temp_b[pl.ds(near, 2 * rows), :]
         stage[0, pl.ds(near, 2 * rows), :128] = total[:, :128] * temp
         stage[0, pl.ds(near, 2 * rows), 128:] = total[:, 128:] * temp
@@ -145,7 +145,7 @@
 
         @pl.when(t + SLOTS < n_tiles)
         def _():
-            w_copy(t + SLOTS).start()
+            w_copy(t + SLOTS).start(priority=1)
         temp = temp_b[...]
         z0 = total[:, :128] * temp
         z1 = total[:, 128:] * temp

time: 111 us -> 107 us (0.964)
  Pallas kernels: 111 us -> 106 us
    pallas_call x1, Pallas kernels: 107 us -> 103 us  [local_step(): pl.pallas_call(functools.partial(head_kernel, n_vp, rows, n_tiles), out_s...]
where the time goes in v4:
time: 107 us
  Pallas kernels  106 us (99%)
    pallas_call x1, Pallas kernels, local_step(): pl.pallas_call(functools.partial(head_kernel, n_vp, rows, n_tiles), out_s...  103 us
    pallas_call x1, Pallas kernels, local_step(): pl.pallas_call(write_kernel, out_shape=(jax.ShapeDtypeStruct(table.shape,...  3.38 us

profile of v4, /device:TPU:0, one launch (start us, length us, event | category | flops | bytes accessed | tf_op | source)
XLA Modules:
  0.0 107.1 jit_solution(7258066082520671930)
XLA Ops:
  0.6 103.1 %shard_map.59 = (f32[64,32768]{1,0:T(8,128)S(1)}, f32[1,256]{1,0:T(1,128)S(1)}) custom-call(bf16[256,12288]{1,0:T(8,128)(2,1)} %h_hbm.1, bf16[12288,8192]{1,0:T(8,128)(2,1)} %w_hbm.1, f32[1,256]{1,0:T(1,128)} %bitcast.3, s32[1,256]{1,0:T(1,128)} %bitcast.4), custom_call_target="tpu_custom_call" | custom-call | tf_op jit(solution)/shard_map/pallas_call | solution.py:340
  103.7 3.4 %shard_map.60 = (f32[64,32768]{1,0:T(8,128)}, f32[1,256]{1,0:T(1,128)}) custom-call(f32[64,32768]{1,0:T(8,128)S(1)} %get-tuple-element.6.tab_ref, f32[1,256]{1,0:T(1,128)S(1)} %get-tuple-element.7.cdf_ref), custom_call_target="tpu_custom_call" | custom-call | tf_op jit(solution)/shard_map/pallas_call | solution.py:375

commit v5 on v4

--- a/solution.py
+++ b/solution.py
@@ -51,7 +51,7 @@
         return pltpu.make_async_copy(h_hbm.at[block, span], h_buf.at[block, span], h_sem.at[part, i])
 
     def w_half(part, i):
-        span, cols = pl.ds(i * piece, piece), pl.ds(part * 128, 128)
+        span, cols = pl.ds(i * piece, piece), pl.ds(0, TILE)
         return pltpu.make_async_copy(w_hbm.at[span, cols], w_buf.at[0, span, cols], w0_sem.at[part, i])
 
     small = (pltpu.make_async_copy(temp_hbm, temp_ref, in_sem.at[0]),
@@ -61,8 +61,6 @@
     for i in range(PIECES):
         w_half(0, i).start(priority=1)
         h_copy(0, i).start(priority=1)
-    for i in range(PIECES):
-        w_half(1, i).start(priority=1)
     for i in range(PIECES):
         h_copy(1, i).start(priority=1)
     for t in range(1, SLOTS):
@@ -100,15 +98,20 @@
         send(t, far1, 2).start()
 
     def half(block, cols, part, wait_h):
-        total = None
+        sums = [None, None]
         for i in range(PIECES):
-            w_half(part, i).wait()
+            if part == 0:
+                w_half(part, i).wait()
             if wait_h:
                 h_copy(0, i).wait()
-            x = jnp.dot(h_buf[pl.ds(block, 2 * rows), i * piece:(i + 1) * piece],
-                        w_buf[0, i * piece:(i + 1) * piece, cols], preferred_element_type=jnp.float32)
-            total = x if i == 0 else total + x
-        stage[0, pl.ds(block, 2 * rows), cols] = total * temp_b[pl.ds(block, 2 * rows), :]
+            for q in range(2):
+                span = slice(i * piece + q * piece // 2, i * piece + (q + 1) * piece // 2)
+                x = jnp.dot(h_buf[pl.ds(block, 2 * rows), span], w_buf[0, span, cols],
+                            preferred_element_type=jnp.float32)
+                sums[q] = x if i == 0 else sums[q] + x
+        temp = temp_b[pl.ds(block, 2 * rows), :]
+        for c in range(0, TILE, 128):
+            stage[0, pl.ds(block, 2 * rows), c:c + 128] = sums[0][:, c:c + 128] * temp + sums[1][:, c:c + 128] * temp
 
     def send_half(part):
         cols = pl.ds(part * 128, 128)
@@ -119,24 +122,23 @@
             device_id=(dp, peer), device_id_type=MESH) for k, peer in enumerate((far0, far1))]
 
     def first_tile():
-        half(far, slice(0, 128), 0, True)
+        half(far, slice(0, TILE), 0, True)
         pl.semaphore_wait(barrier, n_vp - 1)
-        for copy in send_half(0):
-            copy.start()
-        half(far, slice(128, 256), 1, False)
-        total = None
+        for part in range(2):
+            for copy in send_half(part):
+                copy.start()
+        sums = [None, None]
         for i in range(PIECES):
             h_copy(1, i).wait()
-            x = jnp.dot(h_buf[pl.ds(near, 2 * rows), i * piece:(i + 1) * piece],
-                        w_buf[0, i * piece:(i + 1) * piece, :], preferred_element_type=jnp.float32)
-            total = x if i == 0 else total + x
-            if i == 0:
-                for copy in send_half(1):
-                    copy.start()
+            for q in range(2):
+                span = slice(i * piece + q * piece // 2, i * piece + (q + 1) * piece // 2)
+                x = jnp.dot(h_buf[pl.ds(near, 2 * rows), span], w_buf[0, span, :],
+                            preferred_element_type=jnp.float32)
+                sums[q] = x if i == 0 else sums[q] + x
         w_copy(jnp.int32(SLOTS)).start(priority=1)
         temp = temp_b[pl.ds(near, 2 * rows), :]
-        stage[0, pl.ds(near, 2 * rows), :128] = total[:, :128] * temp
-        stage[0, pl.ds(near, 2 * rows), 128:] = total[:, 128:] * temp
+        for c in range(0, TILE, 128):
+            stage[0, pl.ds(near, 2 * rows), c:c + 128] = sums[0][:, c:c + 128] * temp + sums[1][:, c:c + 128] * temp
         statistics(jnp.int32(0), stage[0, :, :128], stage[0, :, 128:])
 
     def tile(t):
@@ -251,7 +253,10 @@
         rest = p - hi.astype(jnp.float32)
         mid = rest.astype(jnp.bfloat16)
         low = (rest - mid.astype(jnp.float32)).astype(jnp.bfloat16)
-        c = jnp.dot(jnp.concatenate([hi, mid, low], axis=1), tri[...], preferred_element_type=jnp.float32)
+        terms = jnp.concatenate([hi, mid, low], axis=1)
+        cut = p.shape[0] // 2
+        c = jnp.concatenate([jnp.dot(terms[:cut], tri[...], preferred_element_type=jnp.float32),
+                             jnp.dot(terms[cut:], tri[...], preferred_element_type=jnp.float32)], axis=0)
         for q, (kind, src, t) in enumerate(items):
             cols = pl.ds(pl.multiple_of(src * local_vocab + t * TILE, TILE), TILE)
             cq = c[q * rows:(q + 1) * rows, :]

time: 107 us -> 106 us (level)
  no operation moved by 1% of the time
where the time goes in v5:
time: 106 us
  Pallas kernels  106 us (100%)
    pallas_call x1, Pallas kernels, local_step(): pl.pallas_call(functools.partial(head_kernel, n_vp, rows, n_tiles), out_s...  102 us
    pallas_call x1, Pallas kernels, local_step(): pl.pallas_call(write_kernel, out_shape=(jax.ShapeDtypeStruct(table.shape,...  3.38 us

profile of v5, /device:TPU:0, one launch (start us, length us, event | category | flops | bytes accessed | tf_op | source)
XLA Modules:
  0.0 106.3 jit_solution(9807678605314209308)
XLA Ops:
  0.6 102.3 %shard_map.59 = (f32[64,32768]{1,0:T(8,128)S(1)}, f32[1,256]{1,0:T(1,128)S(1)}) custom-call(bf16[256,12288]{1,0:T(8,128)(2,1)} %h_hbm.1, bf16[12288,8192]{1,0:T(8,128)(2,1)} %w_hbm.1, f32[1,256]{1,0:T(1,128)} %bitcast.3, s32[1,256]{1,0:T(1,128)} %bitcast.4), custom_call_target="tpu_custom_call" | custom-call | tf_op jit(solution)/shard_map/pallas_call | solution.py:345
  102.9 3.4 %shard_map.60 = (f32[64,32768]{1,0:T(8,128)}, f32[1,256]{1,0:T(1,128)}) custom-call(f32[64,32768]{1,0:T(8,128)S(1)} %get-tuple-element.6.tab_ref, f32[1,256]{1,0:T(1,128)S(1)} %get-tuple-element.7.cdf_ref), custom_call_target="tpu_custom_call" | custom-call | tf_op jit(solution)/shard_map/pallas_call | solution.py:380
